TPU v7x, 128 devices: a 2x2x16 block of a 8x8x16 slice. The times are simulated.
128 devices in a mesh: rep: 4 (over x, y), seq: 16 (over z), tp: 2 (over core).
Axes of the slice: x: 2, y: 2, z: 16, core: 2. Of those that a mesh axis runs over, the one named last changes fastest.
The devices are a block of a 8x8x16 slice.
Arguments:
- prefill_query: bfloat16 [32768, 2048], P(('rep', 'seq'), 'tp'), parts along dimension 0, may hold values from -50 to 50
- prefill_key: bfloat16 [32768, 512], P(('rep', 'seq'), 'tp'), parts along dimension 0, may hold values from -6 to 6
- prefill_value: bfloat16 [32768, 512], P(('rep', 'seq'), 'tp'), parts along dimension 0, may hold values from -6 to 6
- doc_ids: int32 [32768], P('rep'), parts along dimension 0, may hold values from 0 to 3, never falling along the last dimension, each value on 1 to 4096 neighbouring positions
- head_window: int32 [16], P('tp'), may hold values from 1024 to 4096, as said below
- dec_query: bfloat16 [256, 2048], P('rep', 'tp'), parts along dimension 0, may hold values from -50 to 50
- dec_key: bfloat16 [256, 512], P('rep', 'tp'), parts along dimension 0, may hold values from -6 to 6
- dec_value: bfloat16 [256, 512], P('rep', 'tp'), parts along dimension 0, may hold values from -6 to 6
- cache_key: bfloat16 [262144, 512], P(('rep', 'seq'), 'tp'), parts along dimension 0, may hold values from -6 to 6
- cache_value: bfloat16 [262144, 512], P(('rep', 'seq'), 'tp'), parts along dimension 0, may hold values from -6 to 6
- page_order: int32 [2048], P(('rep', 'seq')), parts along dimension 0, may hold values from 0 to 511, each once
- lengths: int32 [256], P('rep'), parts along dimension 0, may hold values from 1 to 1024, 32768 in all
- out_proj: bfloat16 [2048, 4096], P('tp'), may hold values from -0.125 to 0.125
Outputs:
- prompt_out: bfloat16 [32768, 4096], P(('rep', 'seq', 'tp')), parts along dimension 0
- decode_out: bfloat16 [256, 4096], P(('rep', 'tp')), parts along dimension 0
There are 4 independent parts, one for each index of `rep`. A program takes and returns all parts, laid end to end along the dimension named above; an argument that names none is the same for every part. Nothing has to cross between parts.
Inputs may be any that keep to these rules, and one draw needn't show every extreme that they name: `head_window`: some head has window 4096.
All inputs are finite; a program needn't handle non-finite values.
Results may differ from a plain program's by a relative error of at most 0.015.
Values may be sent and summed in bfloat16 or wider, within the bound.
A program may use at most 256 MiB of HBM per device.

v0:
```python
from functools import partial
import math

import jax
import jax.numpy as jnp
from jax import lax
from jax.sharding import PartitionSpec as P

HD = 128
WINDOW = 4096
PAGE = 128


masked_score = -1e30


def in_one_piece(arrays, axis, dim, along):
    ends, at = ([], 0)
    for a in arrays[:-1]:
        at += a.shape[along]
        ends.append(at)
    both = jnp.concatenate(arrays, axis=along)
    return tuple(jnp.split(lax.all_gather(both, axis, axis=dim, tiled=True), ends, axis=along))


def collected_together(array, axis):
    leaves = jax.tree.leaves(array)
    order = sorted(range(len(leaves)), key=lambda k: -leaves[k].size)
    width = (1, *leaves[order[0]].shape)[-1]
    lines = [
        jnp.pad(leaves[k].reshape(-1), (0, -leaves[k].size % width)).reshape(-1, width)
        for k in order
    ]
    both, at, found = (lax.all_gather(jnp.concatenate(lines), axis), 0, {})
    for k, line in zip(order, lines):
        slab = both[:, at : at + len(line)].reshape(len(both), -1)
        found[k] = slab[:, : leaves[k].size].reshape(-1, *leaves[k].shape)
        at += len(line)
    numbers = iter(range(len(leaves)))
    return jax.tree.map(lambda _: found[next(numbers)], array)


def joined(array, axis, combine):
    everything = collected_together(
        jax.tree.map(
            lambda part, kind: part.astype(kind), array, (jnp.bfloat16, jnp.bfloat16, jnp.bfloat16)
        ),
        axis,
    )

    def take(k):
        return jax.tree.map(lambda part, own: part[k].astype(own.dtype), everything, array)

    return lax.fori_loop(
        1, lax.axis_size(axis), lambda k, so_far: combine(so_far, take(k)), take(0)
    )


def in_blocks(array, dim, size):
    before, after = (array.shape[:dim], array.shape[dim + 1 :])
    return jnp.moveaxis(array.reshape(*before, size, -1, *after), dim, 0)


def sent_and_summed(array, axis, dim):
    tiles = in_blocks(array, dim, lax.axis_size(axis))
    arrived = lax.all_to_all(tiles, axis, split_axis=0, concat_axis=0, tiled=True)
    return arrived.astype(jnp.float32).sum(axis=0)


def round_half(values):
    return lax.optimization_barrier(values.astype(jnp.bfloat16)).astype(jnp.float32)


def attend_block(
    carry, piece, start, queries, query_pos, query_doc, doc_ids, windows, scale_factor
):
    key_piece, value_piece = piece
    count_rows = key_piece.shape[0]
    kv_local = windows.shape[0]
    head_dim = key_piece.shape[1] // kv_local
    key_pos = start + jnp.arange(count_rows, dtype=jnp.int32)
    key_doc = lax.dynamic_slice_in_dim(doc_ids, jnp.maximum(start, 0), count_rows, 0)
    gap = query_pos[:, None] - key_pos[None, :]
    allowed = (key_pos[None, :] >= 0) & (gap >= 0) & (query_doc[:, None] == key_doc[None, :])
    allowed = allowed[None, None] & (gap[None, None] < windows[:, :, None, None])
    scores = (
        jnp.einsum(
            "tkgd,skd->kgts",
            queries,
            key_piece.reshape(count_rows, kv_local, head_dim),
            preferred_element_type=jnp.float32,
        )
        * scale_factor
    )
    scores = jnp.where(allowed, scores, masked_score)
    running, totals, accum = carry
    fresh = jnp.maximum(running, jnp.max(scores, axis=-1))
    weights = jnp.where(allowed, jnp.exp(scores - fresh[..., None]), 0.0)
    totals = jnp.sum(weights, axis=-1)
    accum = jnp.einsum(
        "kgts,skd->kgtd",
        weights.astype(jnp.bfloat16),
        value_piece.reshape(count_rows, kv_local, head_dim),
        preferred_element_type=jnp.float32,
    )
    return (fresh, totals, accum)


def window_fold(carry, piece, start, update, my_start, tok_rows):
    piece_rows = piece[0].shape[0]
    needed = min(piece_rows, WINDOW + tok_rows)
    offset = jnp.clip(my_start - WINDOW, 0, piece_rows - needed)
    piece = (
        lax.dynamic_slice_in_dim(piece[0], offset, needed, 0),
        lax.dynamic_slice_in_dim(piece[1], offset, needed, 0),
    )
    start = offset
    return update(carry, piece, start)


def combine_parts(first, second):
    top = jnp.maximum(first[0], second[0])
    left = jnp.exp(first[0] - top)
    right = jnp.exp(second[0] - top)
    return (
        top,
        first[1] * left + second[1] * right,
        first[2] * left[..., None] + second[2] * right[..., None],
    )


def project_rows(rows_matrix, out_proj):
    return jnp.dot(rows_matrix, out_proj, preferred_element_type=jnp.float32)


def on_device(
    prefill_query,
    prefill_key,
    prefill_value,
    doc_ids,
    head_window,
    dec_query,
    dec_key,
    dec_value,
    cache_key,
    cache_value,
    page_order,
    lengths,
    out_proj,
):
    tok_rows = prefill_query.shape[0]
    kv_local = prefill_key.shape[1] // HD
    heads_local = prefill_query.shape[1] // HD
    group_size = heads_local // kv_local
    scale_factor = 1.0 / math.sqrt(HD)
    seq_index = lax.axis_index("seq")
    my_start = seq_index * tok_rows
    queries = prefill_query.reshape(tok_rows, kv_local, group_size, HD)
    query_pos = my_start + jnp.arange(tok_rows, dtype=jnp.int32)
    query_doc = lax.dynamic_slice_in_dim(doc_ids, my_start, tok_rows, 0)
    windows = head_window.reshape(kv_local, group_size)
    update = partial(
        attend_block,
        queries=queries,
        query_pos=query_pos,
        query_doc=query_doc,
        doc_ids=doc_ids,
        windows=windows,
        scale_factor=scale_factor,
    )
    initial = (
        jnp.full((kv_local, group_size, tok_rows), masked_score, jnp.float32),
        jnp.zeros((kv_local, group_size, tok_rows), jnp.float32),
        jnp.zeros((kv_local, group_size, tok_rows, HD), jnp.float32),
    )
    windowed = partial(window_fold, update=update, my_start=my_start, tok_rows=tok_rows)
    carry = windowed(initial, in_one_piece((prefill_key, prefill_value), "seq", 0, 1), jnp.int32(0))
    running, totals, accum = carry
    prompt_attn = (
        (accum / totals[..., None])
        .transpose(2, 0, 1, 3)
        .reshape(tok_rows, heads_local * HD)
        .astype(jnp.bfloat16)
    )
    page_count = page_order.shape[0]
    request_count = dec_query.shape[0]
    pages_request = page_count * lax.axis_size("seq") // request_count
    owner = page_order // pages_request
    slot_index = page_order % pages_request
    page_queries = dec_query[owner].reshape(page_count, kv_local, group_size, HD)
    page_keys = cache_key.reshape(page_count, PAGE, kv_local, HD)
    page_values = cache_value.reshape(page_count, PAGE, kv_local, HD)
    scores = (
        jnp.einsum("pkgd,ptkd->pkgt", page_queries, page_keys, preferred_element_type=jnp.float32)
        * scale_factor
    )
    positions = slot_index[:, None] * PAGE + jnp.arange(PAGE, dtype=jnp.int32)[None, :]
    valid = (positions < lengths[owner][:, None])[:, None, None, :]
    scores = jnp.where(valid, scores, masked_score)
    page_top = jnp.max(scores, axis=-1)
    weights = jnp.where(valid, jnp.exp(scores - page_top[..., None]), 0.0)
    page_total = jnp.sum(weights, axis=-1)
    page_accum = jnp.einsum(
        "pkgt,ptkd->pkgd",
        weights.astype(jnp.bfloat16),
        page_values,
        preferred_element_type=jnp.float32,
    )
    member = owner[None, :] == jnp.arange(request_count, dtype=jnp.int32)[:, None]
    request_top = jnp.max(jnp.where(member[:, :, None, None], page_top[None], masked_score), axis=1)
    rescale = jnp.exp(page_top - request_top[owner])
    member_float = member.astype(jnp.float32)
    request_total = jnp.dot(
        member_float,
        (page_total * rescale).reshape(page_count, -1),
        precision=lax.Precision.HIGHEST,
    ).reshape(request_count, kv_local, group_size)
    request_accum = jnp.dot(
        member_float,
        (page_accum * rescale[..., None]).reshape(page_count, -1),
        precision=lax.Precision.HIGHEST,
    ).reshape(request_count, kv_local, group_size, HD)
    merged = joined((request_top, request_total, request_accum), "seq", combine_parts)
    merged_top, merged_total, merged_accum = merged
    dec_queries = dec_query.reshape(request_count, kv_local, group_size, HD)
    own_scores = (
        jnp.einsum(
            "rkgd,rkd->rkg",
            dec_queries,
            dec_key.reshape(request_count, kv_local, HD),
            preferred_element_type=jnp.float32,
        )
        * scale_factor
    )
    final_top = jnp.maximum(merged_top, own_scores)
    shrink = jnp.exp(merged_top - final_top)
    own_weights = jnp.exp(own_scores - final_top)
    final_total = merged_total * shrink + own_weights
    own_values = dec_value.reshape(request_count, kv_local, 1, HD).astype(jnp.float32)
    final_accum = merged_accum * shrink[..., None] + round_half(own_weights)[..., None] * own_values
    decode_attn = (
        (final_accum / final_total[..., None])
        .reshape(request_count, heads_local * HD)
        .astype(jnp.bfloat16)
    )
    prompt_out = sent_and_summed(
        project_rows(prompt_attn, out_proj).astype(jnp.bfloat16), "tp", 0
    ).astype(jnp.bfloat16)
    decode_out = sent_and_summed(
        project_rows(decode_attn, out_proj).astype(jnp.bfloat16), "tp", 0
    ).astype(jnp.bfloat16)
    return (prompt_out, decode_out)


def solution(mesh):
    placed = (
        P(("rep", "seq"), "tp"),
        P(("rep", "seq"), "tp"),
        P(("rep", "seq"), "tp"),
        P("rep"),
        P("tp"),
        P("rep", "tp"),
        P("rep", "tp"),
        P("rep", "tp"),
        P(("rep", "seq"), "tp"),
        P(("rep", "seq"), "tp"),
        P(("rep", "seq")),
        P("rep"),
        P("tp", None),
    )
    return jax.shard_map(
        on_device,
        mesh=mesh,
        in_specs=placed,
        out_specs=(P(("rep", "seq", "tp"), None), P(("rep", "tp"), None)),
        check_vma=False,
    )
```

profile of v0, /device:TPU:69, one launch (start us, length us, event | category | flops | bytes accessed | tf_op | source)
XLA Modules:
  0.0 345.0 jit_solution(10987832811644913379)
XLA Ops:
  9.7 4.0 %reshape.274 = bf16[32,128,2,128]{3,2,1,0:T(2,128)(2,1)} reshape(bf16[4096,256]{1,0:T(8,128)(2,1)} %param.23) | data formatting | bytes 4194304 | tf_op jit(solution)/shard_map/reshape | solution.py:191
  14.5 2.9 fusion.50
  20.3 2.0 reshape.275
  22.4 2.4 fusion.20
  35.2 4.5 %compare_and_fusion.1 = pred[512,4608]{0,1:T(8,128)(4,1)S(1)} fusion(s32[512]{0:T(512)S(1)} %dynamic_slice.42, s32[4608]{0:T(1024)S(1)} %dynamic_slice.43, pred[4608]{0:T(1024)(128)(4,1)S(1)} %broadcast_compare_fusion, s32[4608]{0:T(1024)S(1)} %iota_add_fusion, s32[512]{0:T(512)S(1)} %iota_add_fusion.1), kind=kLoop, calls=%fused_computation.18 | loop fusion | flops 11796480 | bytes 2404864 | tf_op jit(solution)/shard_map/and | solution.py:84
  39.7 4.6 %broadcast_subtract_fusion = s32[512,4608]{0,1:T(8,128)} fusion(s32[4608]{0:T(1024)S(1)} %iota_add_fusion, s32[512]{0:T(512)S(1)} %iota_add_fusion.1), kind=kLoop, calls=%fused_computation.20 | loop fusion | flops 2359296 | bytes 9457664 | tf_op jit(solution)/shard_map/sub | solution.py:83
  44.4 48.9 %all-gather.6.cloned.1.call-done = bf16[8320,128]{1,0:T(8,128)(2,1)} async-done(((bf16[520,128]{1,0:T(8,128)(2,1)}), bf16[8320,128]{1,0:T(8,128)(2,1)}) %all-gather.6.cloned.1.call-update) | async-done | bytes 2129936 | tf_op jit(solution)/shard_map/all_gather | solution.py:34
  94.2 3.1 slice.41
  100.0 29.9 %while.19 = (s32[]{:T(128)}, f32[64,2,4]{0,2,1:T(4,128)S(1)}, f32[64,2,4]{0,2,1:T(4,128)S(1)}, f32[64,2,4,128]{3,2,1,0:T(4,128)S(1)}, bf16[16,64,2,4]{1,3,2,0:T(...) while((s32[]{:T(128)}, f32[64,2,4]{0,2,1:T(4,128)S(1)}, ...), condition=%wide.region_7.8_spmd, body=%wide.region_6.7_spmd.sunk | while | flops 266245 | bytes 682135 | solution.py:54
  100.3 1.7 fusion.64
  104.3 1.7 fusion.64
  106.3 1.7 fusion.64
  108.3 1.7 fusion.64
  110.3 1.7 fusion.64
  112.3 1.7 fusion.64
  114.2 1.7 fusion.64
  116.2 1.7 fusion.64
  118.2 1.7 fusion.64
  120.2 1.7 fusion.64
  122.2 1.7 fusion.64
  126.2 1.7 fusion.64
  130.9 5.0 %convolution_convert_fusion.1 = bf16[64,4096]{1,0:T(8,128)(2,1)S(1)} fusion(bf16[64,1024]{1,0:T(8,128)(2,1)S(1)} %convert_element_type.136, bf16[1024,4096]{1,0:T(8,128)(2,1)} %param.27), kind=kOutput, calls=%fused_computation.21 | convolution fusion | flops 537133056 | bytes 9043968 | tf_op jit(solution)/shard_map/dot_general | solution.py:133
  135.9 14.2 %all_to_all.10 = bf16[2,32,4096]{2,1,0:T(8,128)(2,1)S(1)} all-to-all(bf16[2,32,4096]{2,1,0:T(8,128)(2,1)S(1)} %bitcast.106), channel_id=1, replica_groups=mesh['rep'=4,'seq'=16,'tp'=2] {'tp'}, dimensions={0} | all-to-all | bytes 1048576 | tf_op jit(solution)/shard_map/all_to_all | solution.py:66
  151.0 52.6 %all-gather.4.cloned.1.call-done = bf16[8192,512]{0,1:T(8,128)(2,1)} async-done(((bf16[512,512]{0,1:T(8,128)(2,1)}), bf16[8192,512]{0,1:T(8,128)(2,1)}) %all-gather.4.cloned.1.call-update) | async-done | bytes 8388624 | tf_op jit(solution)/shard_map/all_gather | solution.py:23
  203.5 3.8 %fusion.48 = (bf16[8192,256]{0,1:T(8,128)(2,1)S(1)}, bf16[8192,256]{0,1:T(8,128)(2,1)S(1)}) fusion(bf16[8192,512]{0,1:T(8,128)(2,1)} %all-gather.4.cloned.1.call-done), kind=kLoop, calls=%fused_computation.83 | loop fusion | bytes 16777216 | tf_op jit(solution)/shard_map/split | solution.py:23
  207.4 5.9 %constant_dynamic-slice_fusion = (bf16[4608,256]{0,1:T(8,128)(2,1)}, bf16[4608,256]{0,1:T(8,128)(2,1)}) fusion(bf16[8192,256]{0,1:T(8,128)(2,1)S(1)} %get-tuple-element.227, s32[]{:T(128)S(6)} %min.4, bf16[8192,256]{0,1:T(8,128)(2,1)S(1)} %get-tuple-element.226), kind=kLoop, calls=%fused_computation.75 | loop fusion | bytes 9437188 | tf_op jit(solution)/shard_map/dynamic_slice | solution.py:115
  213.3 34.8 %fusion.3 = (f32[2,4,512]{2,1,0:T(4,128)S(1)}, f32[2,4608,512,4]{2,1,3,0:T(8,128)}) fusion(s32[2,4]{1,0:T(2,128)S(1)} %lt.65, s32[512,4608]{0,1:T(8,128)} %broadcast_subtract_fusion, pred[512,4608]{0,1:T(8,128)(4,1)S(1)} %compare_and_fusion.1, bf16[4608,2,128,1]{0,2,3,1:T(8,128)(2,1)} %bitcast.98, bf16[512,2,4,128]{3,2,1,0:T(4,128)(2,1)S(1)} %copy-done.2), kind=kOutput, calls=%fused_computation.14 | convolution fusion | flops 4926205952 | bytes 90718240 | tf_op jit(solution)/shard_map/tkgd,skd->kgts/dot_general | solution.py:87
  248.0 31.9 %fusion.6 = f32[2,4,512]{2,1,0:T(4,128)S(1)} fusion(f32[2,4,512]{2,1,0:T(4,128)S(1)} %broadcast_maximum_fusion, f32[2,4608,512,4]{2,1,3,0:T(8,128)} %get-tuple-element.237, s32[2,4]{1,0:T(2,128)S(1)} %lt.65, s32[512,4608]{0,1:T(8,128)} %broadcast_subtract_fusion, pred[512,4608]{0,1:T(8,128)(4,1)S(1)} %compare_and_fusion.1), kind=kLoop, calls=%fused_computation.17 | loop fusion | flops 132116480 | bytes 87326752 | tf_op jit(solution)/shard_map/reduce_sum | solution.py:99
  279.9 36.3 %fusion.7 = bf16[512,2,4,128]{0,3,2,1:T(8,128)(2,1)} fusion(bf16[4608,2,128,1]{0,2,3,1:T(8,128)(2,1)} %bitcast.105, f32[2,4,512]{2,1,0:T(4,128)S(1)} %broadcast_maximum_fusion, f32[2,4608,512,4]{2,1,3,0:T(8,128)} %get-tuple-element.237, s32[2,4]{1,0:T(2,128)S(1)} %lt.65, s32[512,4608]{0,1:T(8,128)} %broadcast_subtract_fusion, ...), kind=kOutput, calls=%fused_computation.23 | convolution fusion | flops 4965007360 | bytes 90734624 | tf_op jit(solution)/shard_map/kgts,skd->kgtd/dot_general | solution.py:100
  316.2 8.3 %convolution_convert_fusion = bf16[512,4096]{1,0:T(8,128)(2,1)S(1)} fusion(bf16[512,1024]{0,1:T(8,128)(2,1)} %bitcast.118, bf16[1024,4096]{1,0:T(8,128)(2,1)} %param.27), kind=kOutput, calls=%fused_computation.19 | convolution fusion | flops 4297064448 | bytes 13631488 | tf_op jit(solution)/shard_map/dot_general | solution.py:133
  324.5 8.6 %all_to_all.11 = bf16[2,256,4096]{2,1,0:T(8,128)(2,1)} all-to-all(bf16[2,256,4096]{2,1,0:T(8,128)(2,1)S(1)} %bitcast.99), channel_id=1, replica_groups=mesh['rep'=4,'seq'=16,'tp'=2] {'tp'}, dimensions={0} | all-to-all | bytes 8388608 | tf_op jit(solution)/shard_map/all_to_all | solution.py:66
  333.2 5.0 %reduce_sum.43 = bf16[256,4096]{1,0:T(8,128)(2,1)} reduce(bf16[2,256,4096]{2,1,0:T(8,128)(2,1)} %all_to_all.11, bf16[]{:T(256)} %constant.95.clone.1), dimensions={0}, to_apply=%region_2.3 | reduce | flops 1048576 | bytes 6291458 | tf_op jit(solution)/shard_map/reduce_sum | solution.py:67
  (130 shorter events, 30.8 us)
Async XLA Ops:
  7.2 6.5 %copy-start = (s32[64]{0:T(128)S(1)}, s32[64]{0:T(128)}, u32[]{:S(2)}) copy-start(s32[64]{0:T(128)} %param.26) | copy-start | bytes 772
  7.2 13.1 %copy-start.4 = (bf16[4096,256]{1,0:T(8,128)(2,1)S(1)}, bf16[4096,256]{1,0:T(8,128)(2,1)}, u32[]{:S(2)}) copy-start(bf16[4096,256]{1,0:T(8,128)(2,1)} %param.24) | copy-start | bytes 6291460
  7.2 86.1 %all-gather.6.cloned.1.call-start = ((), (), s32[]{:S(2)}) async-start(), calls=%async_computation.3 | async-start | bytes 2263040 | tf_op jit(solution)/shard_map/all_gather | solution.py:34
  8.1 9.6 %copy-start.7 = (s32[32]{0:T(128)}, s32[32]{0:T(128)S(1)}, u32[]{:S(2)}) copy-start(s32[32]{0:T(128)S(1)} %get-tuple-element.225) | copy-start | bytes 388
  13.7 15.6 %copy-start.3 = (bf16[64,1024]{1,0:T(8,128)(2,1)S(1)}, bf16[64,1024]{1,0:T(8,128)(2,1)}, u32[]{:S(2)}) copy-start(bf16[64,1024]{1,0:T(8,128)(2,1)} %param.20) | copy-start | bytes 393220
  13.7 18.0 %copy-start.5 = (bf16[512,1024]{1,0:T(8,128)(2,1)S(1)}, bf16[512,1024]{1,0:T(8,128)(2,1)}, u32[]{:S(2)}) copy-start(bf16[512,1024]{1,0:T(8,128)(2,1)} %param.15) | copy-start | bytes 3145732
  17.4 0.7 copy-start.6
  17.8 7.1 %copy-start.8 = (s32[32]{0:T(128)S(1)}, s32[32]{0:T(128)}, u32[]{:S(2)}) copy-start(s32[32]{0:T(128)} %copy-done.7) | copy-start | bytes 388
  26.1 177.4 %all-gather.4.cloned.1.call-start = ((), (), s32[]{:S(2)}) async-start(), calls=%async_computation.2 | async-start | bytes 8912896 | tf_op jit(solution)/shard_map/all_gather | solution.py:23
  207.4 5.9 %copy-start.2 = (bf16[512,2,4,128]{3,2,1,0:T(4,128)(2,1)S(1)}, bf16[512,2,4,128]{3,2,1,0:T(4,128)(2,1)}, u32[]{:S(2)}) copy-start(bf16[512,2,4,128]{3,2,1,0:T(4,128)(2,1)} %reshape.270) | copy-start | bytes 3145732
  316.2 22.0 %copy-start.1 = (s32[64]{0:T(128)S(1)}, s32[64]{0:T(128)}, u32[]{:S(2)}) copy-start(s32[64]{0:T(128)} %param.26) | copy-start | bytes 772
Sparse Core Ops, SparseCore 0:
  26.3 66.9 all-gather.5
  95.0 108.5 all-gather.3
where the time goes:
time: 346 us; the launch traced here: 345 us
  waiting for transfers between devices  102 us (29%)
  matrix products  91.1 us (26%)
  other arithmetic  77 us (22%)
  local copies, waits for them, and re-layouts  37.4 us (11%)
  blocking collectives  22.9 us (7%)
  between operations  14.4 us (4%)
    all_gather x1, waiting for transfers between devices, in_one_piece(): lax.all_gather(both, axis, axis=dim, tiled=True)  52.6 us
    all_gather x1, waiting for transfers between devices, collected_together(): both, at, found = (lax.all_gather(jnp.concatenate(lines), axis), 0, {})  48.9 us
    dot_general x1, matrix products, attend_block(): jnp.einsum('kgts,skd->kgtd', weights.astype(jnp.bfloat16), value_piece.re...  36.3 us
    dot_general x1, matrix products, attend_block(): jnp.einsum('tkgd,skd->kgts', queries, key_piece.reshape(count_rows, kv_lo...  34.8 us
    reduce_sum x1, other arithmetic, attend_block(): totals = jnp.sum(weights, axis=-1)  31.9 us
    add x15, other arithmetic, combine_parts(): first[2] * left[..., None] + second[2] * right[..., None]  25.5 us
    all_to_all x2, blocking collectives, sent_and_summed(): lax.all_to_all(tiles, axis, split_axis=0, concat_axis=0, tiled=True)  22.9 us
    dot_general x2, matrix products, project_rows(): return jnp.dot(rows_matrix, out_proj, preferred_element_type=jnp.float32)  13.3 us
  transfers between devices with their start and end apart: 2, of which 2 were waited for; matrix products, arithmetic and copies ran while one was open for 18% of the time, Pallas kernels for 0%

commit v1 on v0

v1 whole, which is shorter than its diff:
```python
import functools
import math

import jax
import jax.numpy as jnp
from jax import lax
from jax.experimental import pallas as pl
from jax.experimental.pallas import tpu as pltpu
from jax.sharding import PartitionSpec as P

HD = 128
PAGE = 128
MASKED = -1e30
START = -1e29
MESH = pl.DeviceIdType.MESH


def lane_iota(rows):
    return lax.broadcasted_iota(jnp.int32, (rows, 128), 1)


def row_iota(rows):
    return lax.broadcasted_iota(jnp.int32, (rows, 128), 0)


def attention_kernel(
    n,
    q_ref, k_ref, v_ref, doc_ref, hw_ref, dq_ref, dk_ref, dv_ref, ck_hbm, cv_hbm, po_ref, len_ref, w_hbm,
    out_hbm, dout_ref,
    q2_ref, lo_ref, m_ref, l_ref, acc_ref,
    fkv, bkv,
    ck_ref, cv_ref, dq2_ref, dm_ref, dl_ref, dacc_ref,
    obuf, lbuf, orecv, lrecv, dgat,
    w_ref, attn, sent, got, held,
    cache_sem, w_sem, p_send, p_recv, out_sem, f_send, f_recv, b_send, b_recv, a_send, a_recv,
    r_send, r_recv, s_send, s_recv,
):
    me = lax.axis_index("seq")
    core = lax.axis_index("tp")
    right = lax.rem(me + 1, n)
    left = lax.rem(me + n - 1, n)
    tok = q_ref.shape[0]
    heads = q_ref.shape[1] // HD
    kv = k_ref.shape[1] // HD
    group = heads // kv
    reqs = dq_ref.shape[0]
    pages = po_ref.shape[0]
    slots = pages * n // reqs
    hops, front = fkv.shape[1:3]
    legs, back = bkv.shape[1:3]
    piece = front // 2
    drows = reqs * group
    half = tok // 2
    share = drows // n
    scale = math.log2(math.e) / math.sqrt(HD)
    nt = (((1,), (1,)), ((), ()))

    caches = [
        pltpu.make_async_copy(ck_hbm, ck_ref, cache_sem.at[0]),
        pltpu.make_async_copy(cv_hbm, cv_ref, cache_sem.at[1]),
    ]
    for copy in caches:
        copy.start()
    weights_copy = pltpu.make_async_copy(w_hbm, w_ref, w_sem.at[0])
    weights_copy.start()

    barrier = pltpu.get_barrier_semaphore()

    @pl.loop(1, n)
    def _(off):
        pl.semaphore_signal(
            barrier, inc=1, device_id={"seq": lax.rem(me + off, n)}, device_id_type=MESH
        )

    pl.semaphore_signal(barrier, inc=1, device_id={"tp": 1 - core}, device_id_type=MESH)
    pl.semaphore_wait(barrier, n)

    def remote(src, dst, send, recv, to):
        return pltpu.make_async_remote_copy(
            src_ref=src, dst_ref=dst, send_sem=send, recv_sem=recv,
            device_id={"seq": to}, device_id_type=MESH,
        )

    def f_copy(d, u, own=None):
        rows = pl.ds(pl.multiple_of(u // 2 * piece, 16), piece)
        w = lax.rem(u, 2)
        src = fkv.at[w, d - 2, rows] if own is None else own.at[rows]
        return remote(src, fkv.at[w, d - 1, rows], f_send.at[d - 1, u], f_recv.at[d - 1, u], right)

    skip = n - 1 - hops

    def b_copy(h, w):
        return remote(bkv.at[w, h - 2], bkv.at[w, h - 1], b_send.at[h - 1, w], b_recv.at[h - 1, w], left)

    def b_first(w):
        src = (k_ref, v_ref)[w].at[pl.ds(front, back)]
        to = lax.rem(me + n - skip, n)
        return remote(src, bkv.at[w, 0], b_send.at[0, w], b_recv.at[0, w], to)

    for w in range(2):
        b_first(w).start()
    for u in range(4):
        f_copy(1, u, (k_ref, v_ref)[u % 2]).start()

    doc = doc_ref[...]
    row = row_iota(tok)
    qpos = row + me * tok
    first_key = jnp.zeros((tok, 128), jnp.int32)
    for value in range(1, 4):
        below = jnp.where(doc < value, 1.0, 0.0)
        count = jnp.sum(jnp.sum(below, axis=0, keepdims=True), axis=1, keepdims=True)
        begin = jnp.broadcast_to(count, (tok, 128)).astype(jnp.int32)
        first_key = jnp.where(qpos >= begin, begin, first_key)

    def halves(x):
        x = x.astype(jnp.float32) * scale
        high = x.astype(jnp.bfloat16)
        return high, (x - high.astype(jnp.float32)).astype(jnp.bfloat16)

    for h in range(heads):
        rows = pl.ds(h * tok, tok)
        q2_ref[rows, :HD], q2_ref[rows, HD:] = halves(q_ref[:, h * HD : (h + 1) * HD])
        lo_ref[rows] = jnp.maximum(first_key, qpos - hw_ref[h] + 1)
    m_ref[...] = jnp.full(m_ref.shape, START, jnp.float32)
    l_ref[...] = jnp.zeros(l_ref.shape, jnp.float32)
    acc_ref[...] = jnp.zeros(acc_ref.shape, jnp.float32)
    for h in range(heads):
        rows = pl.ds(h * reqs, reqs)
        dq2_ref[rows, :HD], dq2_ref[rows, HD:] = halves(dq_ref[:, h * HD : (h + 1) * HD])
    dm_ref[...] = jnp.full(dm_ref.shape, START, jnp.float32)
    dl_ref[...] = jnp.zeros(dl_ref.shape, jnp.float32)
    dacc_ref[...] = jnp.zeros(dacc_ref.shape, jnp.float32)

    def fold(q2, k, v, masks, m_at, l_at, acc_at):
        keys = k.shape[0]
        s = lax.dot_general(
            q2, jnp.concatenate([k, k], axis=1), nt, preferred_element_type=jnp.float32
        )
        parts = [
            jnp.where(masks[c], s[:, c * 128 : (c + 1) * 128], MASKED) for c in range(keys // 128)
        ]
        top = functools.reduce(jnp.maximum, parts)
        old = m_at[...]
        new = jnp.maximum(old, jnp.max(top, axis=1, keepdims=True))
        alpha = jnp.exp2(old - new)
        weights = [jnp.exp2(part - new) for part in parts]
        m_at[...] = new
        l_at[...] = l_at[...] * alpha + functools.reduce(jnp.add, weights)
        p = jnp.concatenate([w.astype(jnp.bfloat16) for w in weights], axis=1)
        acc_at[...] = acc_at[...] * alpha + jnp.dot(p, v, preferred_element_type=jnp.float32)

    lane = lane_iota(1)
    wide_lane = lane_iota(tok)

    def columns_of(g):
        return pl.ds(pl.multiple_of(g * HD, HD), HD)

    def prompt_fold(j, k, v, places, causal=False):
        for i in range(pair):
            rows = pl.ds(pl.multiple_of((j * pair + i) * tok, tok), tok)
            low = lo_ref[rows]
            masks = []
            for c, place in enumerate(places):
                ok = place >= low
                if causal:
                    ok = ok & (wide_lane + c * 128 <= row)
                masks.append(ok)
            fold(q2_ref[rows], k, v, masks, m_ref.at[rows], l_ref.at[rows], acc_ref.at[rows])

    pair = heads // 4
    per = group // pair

    def own_piece(j):
        places = [lane + (me * tok + c * 128) for c in range(tok // 128)]
        g = j // per
        prompt_fold(j, k_ref[:, head_cols(g)], v_ref[:, head_cols(g)], places, True)

    def placed(starts):
        total = sum(count for count, _ in starts)
        places = []
        for c in range(-(-total // 128)):
            place, at = jnp.full((1, 128), -1, jnp.int32), total
            for count, begin in reversed(starts):
                at -= count
                if at < (c + 1) * 128 and at + count > c * 128:
                    place = jnp.where(lane + c * 128 < at + count, lane + (c * 128 - at) + begin, place)
            places.append(place)
        return places

    def joined(blocks):
        empty = -sum(block.shape[0] for block in blocks) % 128
        return jnp.concatenate(blocks + [jnp.zeros((empty, HD), jnp.bfloat16)], axis=0)

    def tile(j, d, h=None):
        cols = columns_of(j // per)
        starts = [(front, (me - d) * tok)]
        blocks = [[fkv[w, d - 1, :, cols]] for w in range(2)]
        if h is not None:
            for i in range(2):
                starts.append((back, (me - (legs + 1 - h - i)) * tok + front))
                for w in range(2):
                    blocks[w].append(bkv[w, h - 1 + i, :, cols])
        prompt_fold(j, joined(blocks[0]), joined(blocks[1]), placed(starts))

    def head_cols(g):
        return slice(g * HD, (g + 1) * HD)

    dlane = lane_iota(drows)
    drequest = lax.rem(row_iota(drows), reqs)
    step_pages = pages // 8

    def decode_tile(t):
        masks = []
        for i in range(step_pages):
            slot = po_ref[t * step_pages + i]
            owner = slot // slots
            limit = len_ref[owner] - (slot - owner * slots) * PAGE
            masks.append((drequest == owner) & (dlane < limit))
        keys = pl.ds(pl.multiple_of(t * (step_pages * PAGE), PAGE), step_pages * PAGE)
        for g in range(kv):
            rows = pl.ds(g * drows, drows)
            fold(
                dq2_ref[rows], ck_ref[keys, head_cols(g)], cv_ref[keys, head_cols(g)], masks,
                dm_ref.at[rows], dl_ref.at[rows], dacc_ref.at[rows],
            )

    both = kv * share
    diagonal = lane_iota(both) == row_iota(both)

    def a_copies(to, frm):
        return [
            remote(obuf.at[to], orecv.at[frm], a_send.at[to, 0], a_recv.at[frm, 0], to),
            remote(lbuf.at[to], lrecv.at[frm], a_send.at[to, 1], a_recv.at[frm, 1], to),
        ]

    def decode_send():
        for to in range(n):
            outs, tops = [], []
            for g in range(kv):
                rows = pl.ds(g * drows + to * share, share)
                total = jnp.sum(dl_ref[rows], axis=1, keepdims=True)
                some = total > 0.0
                outs.append(jnp.where(some, dacc_ref[rows] / jnp.where(some, total, 1.0), 0.0))
                tops.append(
                    jnp.where(some, dm_ref[rows] + jnp.log2(jnp.where(some, total, 1.0)), MASKED)
                )
            obuf[to] = jnp.concatenate(outs, axis=0).astype(jnp.bfloat16)
            tops = jnp.where(diagonal, jnp.concatenate(tops, axis=0), 0.0)
            lbuf[to] = jnp.sum(tops, axis=0, keepdims=True)
        orecv[me] = obuf[me]
        lrecv[me] = lbuf[me]

    def decode_start():
        @pl.loop(1, n)
        def _(off):
            for copy in a_copies(lax.rem(me + off, n), me):
                copy.start()

    def r_copy(t):
        block = dgat.at[lax.rem(me + n - (t - 1), n)]
        return remote(block, block, r_send.at[t - 1], r_recv.at[t - 1], right)

    def s_copy(t):
        block = dgat.at[lax.rem(me + (t - 1), n)]
        return remote(block, block, s_send.at[t - 1], s_recv.at[t - 1], left)

    def r_arrived(t):
        block = dgat.at[lax.rem(me + n - t, n)]
        remote(block, block, r_send.at[t - 1], r_recv.at[t - 1], right).wait_recv()

    def s_arrived(t):
        block = dgat.at[lax.rem(me + t, n)]
        remote(block, block, s_send.at[t - 1], s_recv.at[t - 1], left).wait_recv()

    def decode_merge():
        @pl.loop(1, n)
        def _(off):
            other = lax.rem(me + off, n)
            for copy in a_copies(other, other):
                copy.wait_recv()
            for copy in a_copies(other, me):
                copy.wait_send()

        tops = []
        for i in range(n):
            spread = jnp.broadcast_to(lrecv[i, 0:1, :], (both, 128))
            tops.append(jnp.sum(jnp.where(diagonal, spread, 0.0), axis=1, keepdims=True))
        request = pl.ds(pl.multiple_of(lax.rem(me * share, reqs), 16), share)
        own_scores, own_values = [], []
        for g in range(kv):
            rows = pl.ds(pl.multiple_of(g * drows + me * share, 16), share)
            q = dq2_ref[rows, :HD].astype(jnp.float32) + dq2_ref[rows, HD:].astype(jnp.float32)
            key = dk_ref[request, head_cols(g)].astype(jnp.float32)
            own_scores.append(jnp.sum(q * key, axis=1, keepdims=True))
            own_values.append(dv_ref[request, head_cols(g)].astype(jnp.float32))
        own_score = jnp.concatenate(own_scores, axis=0)
        peak = functools.reduce(jnp.maximum, tops + [own_score])
        total = jnp.exp2(own_score - peak)
        value = total * jnp.concatenate(own_values, axis=0)
        for i in range(n):
            w = jnp.exp2(tops[i] - peak)
            total = total + w
            value = value + w * orecv[i].astype(jnp.float32)
        dgat[me] = (value / total).astype(jnp.bfloat16)

    far_right, far_left = n // 2, n - 1 - n // 2

    def gather_hop(t):
        r_arrived(t)

        @pl.when(t < far_right)
        def _():
            r_copy(t + 1).start()

        @pl.when(t <= far_left)
        def _():
            s_arrived(t)

            @pl.when(t < far_left)
            def _():
                s_copy(t + 1).start()

    def decode_gather():
        for i in range(n):
            hh, request = divmod(i * share, reqs)
            side, request = divmod(request, reqs // 2)
            for g in range(kv):
                attn[
                    side, pl.ds(half + request, share), pl.ds((g * group + hh) * HD, HD)
                ] = dgat[i, pl.ds(g * share, share)]

    def f_pass(d, u):
        w = lax.rem(u, 2)
        block = fkv.at[w, d - 1, pl.ds(pl.multiple_of(u // 2 * piece, 16), piece)]
        remote(block, block, f_send.at[d - 1, u], f_recv.at[d - 1, u], right).wait_recv()

        @pl.when(d < hops)
        def _():
            f_copy(d + 1, u).start()

    def b_pass(h, w):
        block = bkv.at[w, h - 1]
        remote(block, block, b_send.at[h - 1, w], b_recv.at[h - 1, w], left).wait_recv()

        @pl.when(h < legs)
        def _():
            b_copy(h + 1, w).start()

    for copy in caches:
        copy.wait()
    for half_tiles in range(2):

        @pl.loop(half_tiles * 4, half_tiles * 4 + 4)
        def _(t):
            decode_tile(t)

        f_pass(1, half_tiles)
    for j in range(2):
        own_piece(j)
        f_pass(1, 2 + j)
    decode_send()
    own_piece(2)
    decode_start()
    own_piece(3)

    lag = hops // 2

    @pl.loop(2, hops + 2)
    def _(d):
        @pl.loop(0, 4)
        def _(j):
            @pl.when(d <= hops)
            def _():
                f_pass(d, j)
                h = 2 * (d - lag) + j // 2

                @pl.when(h >= 1)
                def _():
                    b_pass(h, lax.rem(j, 2))

            @pl.when((d >= 4) & (d < 4 + far_right // 2) & (lax.rem(j, 2) == 0))
            def _():
                gather_hop((d - 4) * 2 + j // 2 + 1)

            @pl.when(d <= lag + 1)
            def _():
                tile(j, d - 1)

            @pl.when(d > lag + 1)
            def _():
                tile(j, d - 1, 2 * (d - lag - 1))

            @pl.when((d == 3) & (j == 2))
            def _():
                decode_merge()

            @pl.when((d == 3) & (j == 3))
            def _():
                r_copy(1).start()
                s_copy(1).start()

    decode_gather()
    for w in range(2):
        b_first(w).wait_send()
    for u in range(4):
        f_copy(1, u, (k_ref, v_ref)[u % 2]).wait_send()

    @pl.loop(2, hops + 1)
    def _(d):
        @pl.loop(0, 4)
        def _(u):
            f_copy(d, u).wait_send()

    @pl.loop(2, legs + 1)
    def _(h):
        for w in range(2):
            b_copy(h, w).wait_send()

    @pl.loop(1, far_right + 1)
    def _(t):
        r_copy(t).wait_send()

    @pl.loop(1, far_left + 1)
    def _(t):
        s_copy(t).wait_send()

    for h in range(heads):
        for side in range(2):
            rows = pl.ds(h * tok + side * half, half)
            total = jnp.sum(l_ref[rows], axis=1, keepdims=True)
            attn[side, pl.ds(0, half), pl.ds(h * HD, HD)] = (acc_ref[rows] / total).astype(
                jnp.bfloat16
            )

    weights_copy.wait()
    tiles, _, wide = sent.shape

    def columns(t):
        return pl.ds(pl.multiple_of(t * wide, wide), wide)

    def part(side, t):
        return jnp.dot(attn[side], w_ref[:, columns(t)], preferred_element_type=jnp.float32)

    def p_copy(t):
        return pltpu.make_async_remote_copy(
            src_ref=sent.at[t], dst_ref=got.at[t], send_sem=p_send.at[t], recv_sem=p_recv.at[t],
            device_id={"tp": 1 - core}, device_id_type=MESH,
        )

    def out_copy(t):
        return pltpu.make_async_copy(held.at[t], out_hbm.at[:, columns(t)], out_sem.at[t])

    @pl.loop(0, tiles)
    def _(t):
        sent[t] = part(1 - core, t).astype(jnp.bfloat16)

        @pl.when(t > 0)
        def _():
            p_copy(t - 1).start()

    @pl.loop(0, tiles)
    def _(t):
        own = part(core, t)

        @pl.when(t == 0)
        def _():
            p_copy(tiles - 1).start()

        p_copy(t).wait_recv()
        total = (own + got[t].astype(jnp.float32)).astype(jnp.bfloat16)
        held[t] = total[:half]
        dout_ref[:, columns(t)] = total[half:]

        @pl.when(t > 0)
        def _():
            out_copy(t - 1).start()

    out_copy(tiles - 1).start()

    @pl.loop(0, tiles)
    def _(t):
        p_copy(t).wait_send()
        out_copy(t).wait()


def attend(q, k, v, doc, hw, dq, dk, dv, ck, cv, po, lengths, w):
    n = lax.axis_size("seq")
    tok, width = q.shape
    heads = width // HD
    kv = k.shape[1] // HD
    hops = 4096 // tok
    reqs = dq.shape[0]
    back = 160
    front = tok - back
    legs = hops + 1
    drows = heads * reqs
    share = drows // n
    half, dhalf, out_width = tok // 2, reqs // 2, w.shape[1]
    wide = 512
    tiles = out_width // wide
    bf, f32, i32 = jnp.bfloat16, jnp.float32, jnp.int32
    vm = pl.BlockSpec(memory_space=pltpu.VMEM)
    sm = pl.BlockSpec(memory_space=pltpu.SMEM)
    hbm = pl.BlockSpec(memory_space=pl.ANY)
    dma = pltpu.SemaphoreType.DMA
    return pl.pallas_call(
        functools.partial(attention_kernel, n),
        name="ring_attention",
        out_shape=(
            jax.ShapeDtypeStruct((half, out_width), bf),
            jax.ShapeDtypeStruct((dhalf, out_width), bf),
        ),
        in_specs=[vm, vm, vm, vm, sm, vm, vm, vm, hbm, hbm, sm, sm, hbm],
        out_specs=(hbm, vm),
        scratch_shapes=[
            pltpu.VMEM((heads * tok, 2 * HD), bf),
            pltpu.VMEM((heads * tok, 128), i32),
            pltpu.VMEM((heads * tok, 128), f32),
            pltpu.VMEM((heads * tok, 128), f32),
            pltpu.VMEM((heads * tok, HD), f32),
            pltpu.VMEM((2, hops, front, kv * HD), bf),
            pltpu.VMEM((2, legs, back, kv * HD), bf),
            pltpu.VMEM(ck.shape, bf),
            pltpu.VMEM(cv.shape, bf),
            pltpu.VMEM((drows, 2 * HD), bf),
            pltpu.VMEM((drows, 128), f32),
            pltpu.VMEM((drows, 128), f32),
            pltpu.VMEM((drows, HD), f32),
            pltpu.VMEM((n, share, HD), bf),
            pltpu.VMEM((n, 1, 128), f32),
            pltpu.VMEM((n, share, HD), bf),
            pltpu.VMEM((n, 1, 128), f32),
            pltpu.VMEM((n, share, HD), bf),
            pltpu.VMEM(w.shape, bf),
            pltpu.VMEM((2, half + dhalf, width), bf),
            pltpu.VMEM((tiles, half + dhalf, wide), bf),
            pltpu.VMEM((tiles, half + dhalf, wide), bf),
            pltpu.VMEM((tiles, half, wide), bf),
            dma((2,)),
            dma((1,)),
            dma((tiles,)),
            dma((tiles,)),
            dma((tiles,)),
            dma((hops, 4)),
            dma((hops, 4)),
            dma((legs, 2)),
            dma((legs, 2)),
            dma((n, 2)),
            dma((n, 2)),
            dma((n // 2,)),
            dma((n // 2,)),
            dma((n // 2,)),
            dma((n // 2,)),
        ],
        compiler_params=pltpu.CompilerParams(
            collective_id=0, has_side_effects=True, vmem_limit_bytes=60 * 1024 * 1024
        ),
    )(q, k, v, doc.reshape(-1, 128), hw, dq, dk, dv, ck, cv, po, lengths, w)


def on_device(
    prefill_query,
    prefill_key,
    prefill_value,
    doc_ids,
    head_window,
    dec_query,
    dec_key,
    dec_value,
    cache_key,
    cache_value,
    page_order,
    lengths,
    out_proj,
):
    return attend(
        prefill_query, prefill_key, prefill_value, doc_ids, head_window,
        dec_query, dec_key, dec_value, cache_key, cache_value, page_order, lengths, out_proj,
    )


def solution(mesh):
    placed = (
        P(("rep", "seq"), "tp"),
        P(("rep", "seq"), "tp"),
        P(("rep", "seq"), "tp"),
        P("rep"),
        P("tp"),
        P("rep", "tp"),
        P("rep", "tp"),
        P("rep", "tp"),
        P(("rep", "seq"), "tp"),
        P(("rep", "seq"), "tp"),
        P(("rep", "seq")),
        P("rep"),
        P("tp", None),
    )
    return jax.shard_map(
        on_device,
        mesh=mesh,
        in_specs=placed,
        out_specs=(P(("rep", "seq", "tp"), None), P(("rep", "tp"), None)),
        check_vma=False,
    )
```

time: 346 us -> 120 us (0.35)
  Pallas kernels: 0 us -> 115 us
  waiting for transfers between devices: 102 us -> 0 us
  matrix products: 91.1 us -> 0 us
  other arithmetic: 77 us -> 0 us
  local copies, waits for them, and re-layouts: 37.4 us -> 3.88 us
  blocking collectives: 22.9 us -> 0 us
  between operations: 14.4 us -> 0.65 us
    pallas_call x0 -> x1, Pallas kernels: none -> 115 us  [attend(): pl.pallas_call(functools.partial(attention_kernel, n), name='ring_attenti...]
    all_gather x2 -> x0, waiting for transfers between devices: 102 us -> none  [the longest x1 52.6 us: in_one_piece(): lax.all_gather(both, axis, axis=dim, tiled=True)]
    dot_general x9 -> x0, matrix products: 91.1 us -> none  [the longest x1 36.3 us: attend_block(): jnp.einsum('kgts,skd->kgtd', weights.astype(jnp.bfloat16), value_piece.re...]
    reduce_sum x4 -> x0, other arithmetic: 38 us -> none  [the longest x1 31.9 us: attend_block(): totals = jnp.sum(weights, axis=-1)]
    add x32 -> x0, other arithmetic: 26 us -> none  [the longest x15 25.5 us: combine_parts(): first[2] * left[..., None] + second[2] * right[..., None]]
    all_to_all x2 -> x0, blocking collectives: 22.9 us -> none  [sent_and_summed(): lax.all_to_all(tiles, axis, split_axis=0, concat_axis=0, tiled=True)]
    reshape x8 -> x0, local copies, waits for them, and re-layouts: 8.59 us -> none  [the longest x1 3.96 us: on_device(): page_keys = cache_key.reshape(page_count, PAGE, kv_local, HD)]
    dynamic_slice x3 -> x0, local copies, waits for them, and re-layouts: 7.46 us -> none  [the longest x1 5.89 us: window_fold(): lax.dynamic_slice_in_dim(piece[1], offset, needed, 0)]
  transfers between devices with their start and end apart: 2 -> 0, of which waited for: 2 -> 0; matrix products, arithmetic and copies ran while one was open for 18% -> 0% of each run, Pallas kernels for 0% -> 0%
where the time goes in v1:
time: 120 us
  Pallas kernels  115 us (96%)
  local copies, waits for them, and re-layouts  3.88 us (3%)
    pallas_call x1, Pallas kernels, attend(): pl.pallas_call(functools.partial(attention_kernel, n), name='ring_attenti...  115 us
    unnamed x4, local copies, waits for them, and re-layouts  3.88 us

profile of v1, /device:TPU:69, one launch (start us, length us, event | category | flops | bytes accessed | tf_op | source)
XLA Modules:
  0.0 119.6 jit_solution(6143032351081993012)
XLA Ops:
  0.6 115.1 %ring_attention.1 = (bf16[256,4096]{1,0:T(8,128)(2,1)}, bf16[32,4096]{1,0:T(8,128)(2,1)}) custom-call(bf16[512,1024]{1,0:T(8,128)(2,1)} %q_ref.1, bf16[512,256]{1,0:T(8,128)(2,1)} %k_ref.1, bf16[512,256]{1,0:T(8,128)(2,1)} %v_ref.1, s32[64,128]{1,0:T(8,128)} %bitcast.1, s32[8]{0:T(128)} %hw_ref.1, bf16[64,1024]{1,0:T(8,128)(2,1)} %dq_ref.1, ...), custom_call_target="tpu_custom_call" | custom-call | tf_op jit(solution)/shard_map/ring_attention/pallas_call | solution.py:506
  115.7 0.0 copy-start
  115.7 3.2 %copy.17 = bf16[256,4096]{1,0:T(8,128)(2,1)} copy(bf16[256,4096]{1,0:T(8,128)(2,1)} %get-tuple-element.4) | data formatting | bytes 4194304
  118.9 0.0 copy-done
  118.9 0.7 copy.18
Async XLA Ops:
  115.7 3.2 %copy-start = (bf16[32,4096]{1,0:T(8,128)(2,1)S(1)}, bf16[32,4096]{1,0:T(8,128)(2,1)}, u32[]{:S(2)}) copy-start(bf16[32,4096]{1,0:T(8,128)(2,1)} %get-tuple-element.5) | copy-start | bytes 786436

commit v2 on v1

--- a/solution.py
+++ b/solution.py
@@ -25,20 +25,22 @@
 
 def attention_kernel(
     n,
-    q_ref, k_ref, v_ref, doc_ref, hw_ref, dq_ref, dk_ref, dv_ref, ck_hbm, cv_hbm, po_ref, len_ref, w_hbm,
-    out_hbm, dout_ref,
-    q2_ref, lo_ref, m_ref, l_ref, acc_ref,
+    q_hbm, k_ref, v_ref, doc_ref, hw_ref, dq_ref, dk_ref, dv_ref, ck_hbm, cv_hbm, po_ref, len_ref, w_hbm,
+    out_ref, dout_ref,
+    q_ref, q2_ref, lo_ref, m_ref, l_ref, acc_ref,
     fkv, bkv,
     ck_ref, cv_ref, dq2_ref, dm_ref, dl_ref, dacc_ref,
     obuf, lbuf, orecv, lrecv, dgat,
-    w_ref, attn, sent, got, held,
-    cache_sem, w_sem, p_send, p_recv, out_sem, f_send, f_recv, b_send, b_recv, a_send, a_recv,
+    w_ref, attn, sent, got,
+    q_sem, cache_sem, w_sem, p_send, p_recv, f_send, f_recv, b_send, b_recv, a_send, a_recv,
     r_send, r_recv, s_send, s_recv,
 ):
     me = lax.axis_index("seq")
     core = lax.axis_index("tp")
     right = lax.rem(me + 1, n)
     left = lax.rem(me + n - 1, n)
+    q_copy = pltpu.make_async_copy(q_hbm, q_ref, q_sem.at[0])
+    q_copy.start()
     tok = q_ref.shape[0]
     heads = q_ref.shape[1] // HD
     kv = k_ref.shape[1] // HD
@@ -62,7 +64,6 @@
     for copy in caches:
         copy.start()
     weights_copy = pltpu.make_async_copy(w_hbm, w_ref, w_sem.at[0])
-    weights_copy.start()
 
     barrier = pltpu.get_barrier_semaphore()
 
@@ -89,16 +90,22 @@
 
     skip = n - 1 - hops
 
-    def b_copy(h, w):
-        return remote(bkv.at[w, h - 2], bkv.at[w, h - 1], b_send.at[h - 1, w], b_recv.at[h - 1, w], left)
-
-    def b_first(w):
-        src = (k_ref, v_ref)[w].at[pl.ds(front, back)]
+    def b_rows(u):
+        return pl.ds(pl.multiple_of(u // 2 * (back // 2), 8), back // 2)
+
+    def b_copy(h, u):
+        w, rows = lax.rem(u, 2), b_rows(u)
+        src, dst = bkv.at[w, h - 2, rows], bkv.at[w, h - 1, rows]
+        return remote(src, dst, b_send.at[h - 1, u], b_recv.at[h - 1, u], left)
+
+    def b_first(u):
+        src = (k_ref, v_ref)[u % 2].at[pl.ds(front + u // 2 * (back // 2), back // 2)]
+        dst = bkv.at[u % 2, 0, pl.ds(u // 2 * (back // 2), back // 2)]
         to = lax.rem(me + n - skip, n)
-        return remote(src, bkv.at[w, 0], b_send.at[0, w], b_recv.at[0, w], to)
-
-    for w in range(2):
-        b_first(w).start()
+        return remote(src, dst, b_send.at[0, u], b_recv.at[0, u], to)
+
+    for u in range(4):
+        b_first(u).start()
     for u in range(4):
         f_copy(1, u, (k_ref, v_ref)[u % 2]).start()
 
@@ -117,6 +124,7 @@
         high = x.astype(jnp.bfloat16)
         return high, (x - high.astype(jnp.float32)).astype(jnp.bfloat16)
 
+    q_copy.wait()
     for h in range(heads):
         rows = pl.ds(h * tok, tok)
         q2_ref[rows, :HD], q2_ref[rows, HD:] = halves(q_ref[:, h * HD : (h + 1) * HD])
@@ -189,14 +197,15 @@
 
     def joined(blocks):
         empty = -sum(block.shape[0] for block in blocks) % 128
-        return jnp.concatenate(blocks + [jnp.zeros((empty, HD), jnp.bfloat16)], axis=0)
-
-    def tile(j, d, h=None):
+        rest = [jnp.zeros((empty, HD), jnp.bfloat16)] if empty else []
+        return jnp.concatenate(blocks + rest, axis=0)
+
+    def tile(j, d, h=None, count=0):
         cols = columns_of(j // per)
         starts = [(front, (me - d) * tok)]
         blocks = [[fkv[w, d - 1, :, cols]] for w in range(2)]
-        if h is not None:
-            for i in range(2):
+        if count:
+            for i in range(count):
                 starts.append((back, (me - (legs + 1 - h - i)) * tok + front))
                 for w in range(2):
                     blocks[w].append(bkv[w, h - 1 + i, :, cols])
@@ -338,30 +347,36 @@
         def _():
             f_copy(d + 1, u).start()
 
-    def b_pass(h, w):
-        block = bkv.at[w, h - 1]
-        remote(block, block, b_send.at[h - 1, w], b_recv.at[h - 1, w], left).wait_recv()
+    def b_pass(h, u):
+        block = bkv.at[lax.rem(u, 2), h - 1, b_rows(u)]
+        remote(block, block, b_send.at[h - 1, u], b_recv.at[h - 1, u], left).wait_recv()
 
         @pl.when(h < legs)
         def _():
-            b_copy(h + 1, w).start()
-
+            b_copy(h + 1, u).start()
+
+    own_piece(0)
+    own_piece(1)
+    f_pass(1, 0)
+    own_piece(2)
+    own_piece(3)
+    f_pass(1, 1)
     for copy in caches:
         copy.wait()
-    for half_tiles in range(2):
-
-        @pl.loop(half_tiles * 4, half_tiles * 4 + 4)
+    weights_copy.start()
+    for u in range(2, 4):
+
+        @pl.loop(2 * u - 4, 2 * u - 2)
         def _(t):
             decode_tile(t)
 
-        f_pass(1, half_tiles)
-    for j in range(2):
-        own_piece(j)
-        f_pass(1, 2 + j)
+        f_pass(1, u)
+
+    @pl.loop(4, 8)
+    def _(t):
+        decode_tile(t)
+
     decode_send()
-    own_piece(2)
-    decode_start()
-    own_piece(3)
 
     lag = hops // 2
 
@@ -369,26 +384,35 @@
     def _(d):
         @pl.loop(0, 4)
         def _(j):
+            @pl.when((d == 2) & (j == 1))
+            def _():
+                decode_start()
+
             @pl.when(d <= hops)
             def _():
                 f_pass(d, j)
-                h = 2 * (d - lag) + j // 2
-
-                @pl.when(h >= 1)
+                h = 2 * (d - lag) + j // 2 + 1
+
+                @pl.when((h >= 1) & (h <= legs))
                 def _():
-                    b_pass(h, lax.rem(j, 2))
+                    b_pass(h, lax.rem(j, 2) * 2)
+                    b_pass(h, lax.rem(j, 2) * 2 + 1)
 
             @pl.when((d >= 4) & (d < 4 + far_right // 2) & (lax.rem(j, 2) == 0))
             def _():
                 gather_hop((d - 4) * 2 + j // 2 + 1)
 
-            @pl.when(d <= lag + 1)
+            @pl.when(d <= lag)
             def _():
                 tile(j, d - 1)
 
-            @pl.when(d > lag + 1)
-            def _():
-                tile(j, d - 1, 2 * (d - lag - 1))
+            @pl.when((d == lag + 1) | (d == hops + 1))
+            def _():
+                tile(j, d - 1, 2 + (legs - 2) * (d // (hops + 1)), 1)
+
+            @pl.when((d > lag + 1) & (d <= hops))
+            def _():
+                tile(j, d - 1, 2 * (d - lag) - 1, 2)
 
             @pl.when((d == 3) & (j == 2))
             def _():
@@ -400,8 +424,8 @@
                 s_copy(1).start()
 
     decode_gather()
-    for w in range(2):
-        b_first(w).wait_send()
+    for u in range(4):
+        b_first(u).wait_send()
     for u in range(4):
         f_copy(1, u, (k_ref, v_ref)[u % 2]).wait_send()
 
@@ -413,8 +437,8 @@
 
     @pl.loop(2, legs + 1)
     def _(h):
-        for w in range(2):
-            b_copy(h, w).wait_send()
+        for u in range(4):
+            b_copy(h, u).wait_send()
 
     @pl.loop(1, far_right + 1)
     def _(t):
@@ -447,9 +471,6 @@
             device_id={"tp": 1 - core}, device_id_type=MESH,
         )
 
-    def out_copy(t):
-        return pltpu.make_async_copy(held.at[t], out_hbm.at[:, columns(t)], out_sem.at[t])
-
     @pl.loop(0, tiles)
     def _(t):
         sent[t] = part(1 - core, t).astype(jnp.bfloat16)
@@ -468,19 +489,12 @@
 
         p_copy(t).wait_recv()
         total = (own + got[t].astype(jnp.float32)).astype(jnp.bfloat16)
-        held[t] = total[:half]
+        out_ref[:, columns(t)] = total[:half]
         dout_ref[:, columns(t)] = total[half:]
-
-        @pl.when(t > 0)
-        def _():
-            out_copy(t - 1).start()
-
-    out_copy(tiles - 1).start()
 
     @pl.loop(0, tiles)
     def _(t):
         p_copy(t).wait_send()
-        out_copy(t).wait()
 
 
 def attend(q, k, v, doc, hw, dq, dk, dv, ck, cv, po, lengths, w):
@@ -496,7 +510,7 @@
     drows = heads * reqs
     share = drows // n
     half, dhalf, out_width = tok // 2, reqs // 2, w.shape[1]
-    wide = 512
+    wide = 1024
     tiles = out_width // wide
     bf, f32, i32 = jnp.bfloat16, jnp.float32, jnp.int32
     vm = pl.BlockSpec(memory_space=pltpu.VMEM)
@@ -507,12 +521,13 @@
         functools.partial(attention_kernel, n),
         name="ring_attention",
         out_shape=(
-            jax.ShapeDtypeStruct((half, out_width), bf),
-            jax.ShapeDtypeStruct((dhalf, out_width), bf),
+            pltpu.VMEM((half, out_width), bf),
+            pltpu.VMEM((dhalf, out_width), bf),
         ),
-        in_specs=[vm, vm, vm, vm, sm, vm, vm, vm, hbm, hbm, sm, sm, hbm],
-        out_specs=(hbm, vm),
+        in_specs=[hbm, vm, vm, vm, sm, vm, vm, vm, hbm, hbm, sm, sm, hbm],
+        out_specs=(vm, vm),
         scratch_shapes=[
+            pltpu.VMEM((tok, width), bf),
             pltpu.VMEM((heads * tok, 2 * HD), bf),
             pltpu.VMEM((heads * tok, 128), i32),
             pltpu.VMEM((heads * tok, 128), f32),
@@ -535,16 +550,15 @@
             pltpu.VMEM((2, half + dhalf, width), bf),
             pltpu.VMEM((tiles, half + dhalf, wide), bf),
             pltpu.VMEM((tiles, half + dhalf, wide), bf),
-            pltpu.VMEM((tiles, half, wide), bf),
+            dma((1,)),
             dma((2,)),
             dma((1,)),
             dma((tiles,)),
             dma((tiles,)),
-            dma((tiles,)),
             dma((hops, 4)),
             dma((hops, 4)),
-            dma((legs, 2)),
-            dma((legs, 2)),
+            dma((legs, 4)),
+            dma((legs, 4)),
             dma((n, 2)),
             dma((n, 2)),
             dma((n // 2,)),

time: 120 us -> 113 us (0.942)
  Pallas kernels: 115 us -> 110 us
  local copies, waits for them, and re-layouts: 3.88 us -> 2.02 us
    pallas_call x1, Pallas kernels: 115 us -> 110 us  [attend(): pl.pallas_call(functools.partial(attention_kernel, n), name='ring_attenti...]
    unnamed x4 -> x2, local copies, waits for them, and re-layouts: 3.88 us -> 2.02 us
where the time goes in v2:
time: 113 us
  Pallas kernels  110 us (97%)
  local copies, waits for them, and re-layouts  2.02 us (2%)
    pallas_call x1, Pallas kernels, attend(): pl.pallas_call(functools.partial(attention_kernel, n), name='ring_attenti...  110 us

profile of v2, /device:TPU:69, one launch (start us, length us, event | category | flops | bytes accessed | tf_op | source)
XLA Modules:
  0.0 113.2 jit_solution(10470444069485419776)
XLA Ops:
  0.6 110.5 %ring_attention.1 = (bf16[256,4096]{1,0:T(8,128)(2,1)S(1)}, bf16[32,4096]{1,0:T(8,128)(2,1)S(1)}) custom-call(bf16[512,1024]{1,0:T(8,128)(2,1)} %q_hbm.1, bf16[512,256]{1,0:T(8,128)(2,1)} %k_ref.1, bf16[512,256]{1,0:T(8,128)(2,1)} %v_ref.1, s32[64,128]{1,0:T(8,128)} %bitcast.1, s32[8]{0:T(128)} %hw_ref.1, bf16[64,1024]{1,0:T(8,128)(2,1)} %dq_ref.1, ...), custom_call_target="tpu_custom_call" | custom-call | tf_op jit(solution)/shard_map/ring_attention/pallas_call | solution.py:520
  111.1 1.3 %copy.17 = bf16[256,4096]{1,0:T(8,128)(2,1)} copy(bf16[256,4096]{1,0:T(8,128)(2,1)S(1)} %get-tuple-element.2) | data formatting | bytes 4194304
  112.5 0.7 copy.18
